TPU v7x, 512 devices: a whole 4x8x8 slice. The times are simulated.
512 devices in a mesh: tok: 8 (over x, core), voc: 64 (over z, y).
Axes of the slice: x: 4, y: 8, z: 8, core: 2. Of those that a mesh axis runs over, the one named last changes fastest.
Arguments:
- hidden: bfloat16 [1024, 4608], P(('tok', 'voc')), may hold values from -6 to 6
- norm_gain: float32 [4608], replicated, may hold values from 0.25 to 1.75
- head_weight: bfloat16 [262144, 4608], P(('tok', 'voc')), may hold values from -0.26367188 to 0.26367188
- targets: int32 [1024], replicated, may hold values from 0 to 262143
- lengths: int32 [32], replicated, may hold values from 1 to 32
Outputs:
- token_loss: float32 [1024], P(('tok', 'voc'))
- mean_loss: float32 [], replicated
All inputs are finite; a program needn't handle non-finite values.
Results may differ from a plain program's by a relative error of at most 0.00051.
Values may be sent and summed in bfloat16 or wider, within the bound.
No kernel may reach another device: no remote copies, remote signals or barrier semaphores. Data moves between devices by JAX's collectives and lax.ppermute only.
A program may use at most 64 MiB of HBM per device.

v0:
```python
import functools
import jax
import jax.numpy as jnp
from jax import lax
from jax.sharding import Mesh
from jax.sharding import PartitionSpec as P

WINDOW = 32
TOK_VOC = ("tok_0", "tok_1", "voc_0", "voc_1")
VOC = ("voc_0", "voc_1")
TOK = ("tok_0", "tok_1")


def laid_out(parts, dim):
    lengths = list(parts.shape[1:])
    lengths[dim] *= parts.shape[0]
    return jnp.moveaxis(parts, 0, dim).reshape(lengths)


def gather_in_order(value, axes, turns):
    parts = value[None]
    for k in turns:
        parts = lax.all_gather(parts, axes[k], axis=0, tiled=True)
    held = [lax.axis_size(axes[k]) for k in reversed(turns)]
    parts = parts.reshape(*held, *value.shape)
    turned = sorted(range(len(turns)), key=lambda place: turns[len(turns) - 1 - place])
    return parts.transpose(*turned, *range(len(turns), parts.ndim)).reshape(-1, *value.shape)


def gather_axes(value, axes, turns, dim):
    return laid_out(gather_in_order(value, axes, turns), dim)


def over_axes(value, axes):
    return functools.reduce(lax.psum, axes, value)


def body(hidden, norm_gain, head_weight, targets, lengths):
    own_rows = hidden.shape[0]
    vocab_rows = head_weight.shape[0]
    everyone = lax.axis_size(TOK_VOC)
    whole = own_rows * everyone
    window = WINDOW
    me = lax.axis_index(TOK_VOC)
    values = hidden.astype(jnp.float32)
    meansq = jnp.mean(values * values, axis=1, keepdims=True)
    normed = (values * lax.rsqrt(meansq + 1e-06) * norm_gain[None, :]).astype(jnp.bfloat16)
    offset = me * vocab_rows
    column = jnp.arange(vocab_rows, dtype=jnp.int32)
    grouped = gather_axes(normed, VOC, (0, 1), 0)
    logits = lax.dot_general(
        lax.all_gather(grouped, TOK, axis=0, tiled=True),
        head_weight,
        (((1,), (1,)), ((), ())),
        preferred_element_type=jnp.float32,
    )
    capped = 30.0 * jnp.tanh(logits / 30.0)
    expsum = jnp.sum(jnp.exp(capped), axis=1)
    wanted = targets - offset
    match = column[None, :] == wanted[:, None]
    picked = jnp.sum(jnp.where(match, capped, jnp.zeros_like(capped)), axis=1)
    stats = jnp.stack([expsum, picked])
    position = jnp.arange(window, dtype=jnp.int32)
    live_all = (position[None, :] < lengths[:, None]).astype(jnp.float32).reshape(whole)
    count = jnp.sum(lengths.astype(jnp.float32))
    totals = over_axes(stats, TOK_VOC)
    loss_all = live_all * (jnp.log(totals[0]) - totals[1])
    mean_loss = jnp.sum(loss_all) / count
    token_loss = lax.dynamic_slice_in_dim(loss_all, me * own_rows, own_rows, 0)
    return (token_loss, mean_loss)


def solution(mesh):
    split = Mesh(mesh.devices.reshape(4, 2, 8, 8), ("tok_0", "tok_1", "voc_0", "voc_1"))
    in_specs = (P(TOK_VOC, None), P(), P(TOK_VOC, None), P(), P())
    out_specs = (P(TOK_VOC), P())
    return jax.shard_map(body, mesh=split, in_specs=in_specs, out_specs=out_specs, check_vma=False)
```

profile of v0, /device:TPU:2, one launch (start us, length us, event | category | flops | bytes accessed | tf_op | source)
XLA Modules:
  0.0 209.9 jit_solution(8907988233021880840)
XLA Ops:
  7.2 0.0 all-gather.5.cloned.1.call-start
  7.2 0.9 fusion
  8.1 0.8 fusion.3
  8.9 33.0 %all-gather.1 = bf16[8,2,4608]{2,1,0:T(2,128)(2,1)} all-gather(bf16[1,2,4608]{2,1,0:T(2,128)(2,1)S(1)} %fusion.3), channel_id=2, replica_groups=mesh['tok_0'=4,'tok_1'=2,'voc_0'=8,'voc_1'=8] {'voc_0'}, dimensions={0}, use_global_device_ids=true | all-gather | bytes 165888 | tf_op jit(solution)/shard_map/all_gather | solution.py:23
  41.9 0.0 all-gather.5.cloned.1.call-update
  42.0 0.0 all-gather.7.cloned.1.call-start
  42.0 39.3 %all-gather.5.cloned.1.call-done = bf16[64,2,4608]{2,1,0:T(2,128)(2,1)} async-done(((bf16[8,2,4608]{2,1,0:T(2,128)(2,1)}), bf16[64,2,4608]{2,1,0:T(2,128)(2,1)}) %all-gather.5.cloned.1.call-update) | async-done | bytes 1179664 | tf_op jit(solution)/shard_map/all_gather | solution.py:23
  81.3 2.1 copy.11
  83.4 0.0 copy-start.1
  83.4 0.0 copy-start
  83.4 1.3 reshape_reshape.3
  84.7 0.0 all-gather.7.cloned.1.call-update
  84.7 0.0 copy-done.1
  84.7 0.1 iota_compare_fusion.1
  84.8 0.1 lt.34
  84.9 0.1 lt.32
  85.0 0.7 convert_reduce_fusion
  85.7 0.0 copy-done
  85.7 56.9 %all-gather.7.cloned.1.call-done = bf16[1024,4608]{1,0:T(8,128)(2,1)} async-done(((bf16[128,4608]{1,0:T(8,128)(2,1)}), bf16[1024,4608]{1,0:T(8,128)(2,1)}) %all-gather.7.cloned.1.call-update) | async-done | bytes 9437200 | tf_op jit(solution)/shard_map/all_gather | solution.py:52
  142.6 9.5 %exponential_reduce_fusion = (f32[1024]{0:T(1024)S(1)}, f32[1024]{0:T(1024)S(1)}) fusion(s32[1024]{0:T(1024)S(1)} %broadcast_subtract_fusion, bf16[1024,4608]{1,0:T(8,128)(2,1)} %all-gather.7.cloned.1.call-done, bf16[512,4608]{1,0:T(8,128)(2,1)} %param.7), kind=kOutput, calls=%fused_computation.2 | convolution fusion | flops 4834981888 | bytes 14168064 | tf_op jit(solution)/shard_map/dot_general | solution.py:51
  152.1 9.1 %psum.28 = f32[2,1024]{1,0:T(2,128)S(1)} all-reduce(f32[2,1024]{1,0:T(2,128)S(1)} %pad_maximum_fusion), channel_id=1, replica_groups=mesh['tok_0'=4,'tok_1'=2,'voc_0'=8,'voc_1'=8] {'tok_0'}, use_global_device_ids=true, to_apply=%region_3.4 | all-reduce | flops 2048 | bytes 16384 | tf_op jit(solution)/shard_map/psum | solution.py:35
  161.2 2.5 %psum.29 = f32[2,1024]{1,0:T(2,128)S(1)} all-reduce(f32[2,1024]{1,0:T(2,128)S(1)} %psum.28), channel_id=1, replica_groups=mesh['tok_0'=4,'tok_1'=2,'voc_0'=8,'voc_1'=8] {'tok_1'}, use_global_device_ids=true, to_apply=%region_4.5 | all-reduce | flops 2048 | bytes 16384 | tf_op jit(solution)/shard_map/psum | solution.py:35
  163.7 18.3 %psum.30 = f32[2,1024]{1,0:T(2,128)S(1)} all-reduce(f32[2,1024]{1,0:T(2,128)S(1)} %psum.29), channel_id=1, replica_groups=mesh['tok_0'=4,'tok_1'=2,'voc_0'=8,'voc_1'=8] {'voc_0'}, use_global_device_ids=true, to_apply=%region_5.6 | all-reduce | flops 2048 | bytes 16384 | tf_op jit(solution)/shard_map/psum | solution.py:35
  182.1 17.2 %psum.31 = f32[2,1024]{1,0:T(2,128)S(1)} all-reduce(f32[2,1024]{1,0:T(2,128)S(1)} %psum.30), channel_id=1, replica_groups=mesh['tok_0'=4,'tok_1'=2,'voc_0'=8,'voc_1'=8] {'voc_1'}, use_global_device_ids=true, to_apply=%region_6.7 | all-reduce | flops 2048 | bytes 16384 | tf_op jit(solution)/shard_map/psum | solution.py:35
  199.3 0.6 select_reduce_fusion.1
  199.9 0.6 dynamic_slice.3
  (4 shorter events, 0.0 us)
Async XLA Ops:
  7.2 74.1 %all-gather.5.cloned.1.call-start = ((), (), s32[]{:S(2)}) async-start(), calls=%async_computation | async-start | bytes 1327104 | tf_op jit(solution)/shard_map/all_gather | solution.py:23
  42.0 100.6 %all-gather.7.cloned.1.call-start = ((), (), s32[]{:S(2)}) async-start(), calls=%async_computation.1 | async-start | bytes 10616832 | tf_op jit(solution)/shard_map/all_gather | solution.py:52
  83.4 1.3 copy-start.1
  83.4 2.3 %copy-start = (s32[1024]{0:T(1024)S(1)}, s32[1024]{0:T(1024)}, u32[]{:S(2)}) copy-start(s32[1024]{0:T(1024)} %param.8) | copy-start | bytes 12292
Sparse Core Ops, SparseCore 0:
  42.1 39.1 all-gather.4
  84.8 57.7 all-gather.6
where the time goes:
time: 210 us
  waiting for transfers between devices  96.3 us (46%)
  blocking collectives  80.2 us (38%)
  between operations  16.6 us (8%)
  matrix products  9.45 us (4%)
  local copies, waits for them, and re-layouts  4.13 us (2%)
  other arithmetic  3.11 us (1%)
    all_gather x1, waiting for transfers between devices, body(): lax.all_gather(grouped, TOK, axis=0, tiled=True)  56.9 us
    psum x4, blocking collectives, over_axes(): return functools.reduce(lax.psum, axes, value)  47.2 us
    all_gather x1, waiting for transfers between devices, gather_in_order(): parts = lax.all_gather(parts, axes[k], axis=0, tiled=True)  39.3 us
    all_gather x1, blocking collectives, gather_in_order(): parts = lax.all_gather(parts, axes[k], axis=0, tiled=True)  33 us
    dot_general x1, matrix products, body(): lax.dot_general(lax.all_gather(grouped, TOK, axis=0, tiled=True), head_we...  9.45 us
  transfers between devices with their start and end apart: 2, of which 2 were waited for; matrix products, arithmetic and copies ran while one was open for 0% of the time, Pallas kernels for 0%

commit v1 on v0

--- a/solution.py
+++ b/solution.py
@@ -20,7 +20,9 @@
 def gather_in_order(value, axes, turns):
     parts = value[None]
     for k in turns:
-        parts = lax.all_gather(parts, axes[k], axis=0, tiled=True)
+        parts = jnp.concatenate(
+            lax.all_to_all(jnp.stack([parts] * lax.axis_size(axes[k])), axes[k], 0, 0), axis=0
+        )
     held = [lax.axis_size(axes[k]) for k in reversed(turns)]
     parts = parts.reshape(*held, *value.shape)
     turned = sorted(range(len(turns)), key=lambda place: turns[len(turns) - 1 - place])

time: 210 us -> 186 us (0.89)
  waiting for transfers between devices: 96.3 us -> 49.7 us
  blocking collectives: 80.2 us -> 103 us
    all_to_all x0 -> x2, blocking collectives: none -> 56.2 us  [gather_in_order(): lax.all_to_all(jnp.stack([parts] * lax.axis_size(axes[k])), axes[k], 0, 0)]
    all_gather x1 -> x0, waiting for transfers between devices: 39.3 us -> none  [gather_in_order(): parts = lax.all_gather(parts, axes[k], axis=0, tiled=True)]
    all_gather x1 -> x0, blocking collectives: 33 us -> none  [gather_in_order(): parts = lax.all_gather(parts, axes[k], axis=0, tiled=True)]
    all_gather x1, waiting for transfers between devices: 56.9 us -> 49.7 us  [body(): lax.all_gather(grouped, TOK, axis=0, tiled=True)]
  transfers between devices with their start and end apart: 2 -> 1, of which waited for: 2 -> 1; matrix products, arithmetic and copies ran while one was open for 0% -> 1% of each run, Pallas kernels for 0% -> 0%
where the time goes in v1:
time: 186 us
  blocking collectives  103 us (55%)
  waiting for transfers between devices  49.7 us (27%)
  between operations  16.6 us (9%)
  matrix products  9.46 us (5%)
  local copies, waits for them, and re-layouts  3.55 us (2%)
  other arithmetic  3.11 us (2%)
    all_to_all x2, blocking collectives, gather_in_order(): lax.all_to_all(jnp.stack([parts] * lax.axis_size(axes[k])), axes[k], 0, 0)  56.2 us
    all_gather x1, waiting for transfers between devices, body(): lax.all_gather(grouped, TOK, axis=0, tiled=True)  49.7 us
    psum x4, blocking collectives, over_axes(): return functools.reduce(lax.psum, axes, value)  47.2 us
    dot_general x1, matrix products, body(): lax.dot_general(lax.all_gather(grouped, TOK, axis=0, tiled=True), head_we...  9.46 us
  transfers between devices with their start and end apart: 1, of which 1 were waited for; matrix products, arithmetic and copies ran while one was open for 1% of the time, Pallas kernels for 0%

profile of v1, /device:TPU:2, one launch (start us, length us, event | category | flops | bytes accessed | tf_op | source)
XLA Modules:
  0.0 185.9 jit_solution(18204719648632586857)
XLA Ops:
  7.2 0.0 all-gather.2.cloned.1.call-start
  7.2 0.9 fusion
  8.1 0.8 fusion.2
  8.9 0.1 stack.15
  9.0 19.5 %all_to_all.10 = bf16[8,1,2,4608]{3,2,1,0:T(2,128)(2,1)S(1)} all-to-all(bf16[8,1,2,4608]{3,2,1,0:T(2,128)(2,1)S(1)} %stack.15), channel_id=1, replica_groups=mesh['tok_0'=4,'tok_1'=2,'voc_0'=8,'voc_1'=8] {'voc_0'}, dimensions={0} | all-to-all | bytes 294912 | tf_op jit(solution)/shard_map/all_to_all | solution.py:24
  28.6 0.6 stack.16
  29.2 36.6 %all_to_all.11 = bf16[8,8,2,4608]{3,2,1,0:T(2,128)(2,1)S(1)} all-to-all(bf16[8,8,2,4608]{3,2,1,0:T(2,128)(2,1)S(1)} %stack.16), channel_id=1, replica_groups=mesh['tok_0'=4,'tok_1'=2,'voc_0'=8,'voc_1'=8] {'voc_1'}, dimensions={0} | all-to-all | bytes 2359296 | tf_op jit(solution)/shard_map/all_to_all | solution.py:24
  65.8 0.8 copy.8
  66.6 0.0 copy-start.1
  66.6 0.0 copy-start
  66.7 1.3 reshape_reshape.3
  67.9 0.0 all-gather.2.cloned.1.call-update
  68.0 0.0 copy-done.1
  68.0 0.1 iota_compare_fusion.1
  68.0 0.1 lt.34
  68.1 0.1 lt.32
  68.2 0.7 convert_reduce_fusion
  68.9 0.0 copy-done
  68.9 49.7 %all-gather.2.cloned.1.call-done = bf16[1024,4608]{1,0:T(8,128)(2,1)} async-done(((bf16[128,4608]{1,0:T(8,128)(2,1)}), bf16[1024,4608]{1,0:T(8,128)(2,1)}) %all-gather.2.cloned.1.call-update) | async-done | bytes 9437200 | tf_op jit(solution)/shard_map/all_gather | solution.py:54
  118.6 9.5 %exponential_reduce_fusion = (f32[1024]{0:T(1024)S(1)}, f32[1024]{0:T(1024)S(1)}) fusion(s32[1024]{0:T(1024)S(1)} %broadcast_subtract_fusion, bf16[1024,4608]{1,0:T(8,128)(2,1)} %all-gather.2.cloned.1.call-done, bf16[512,4608]{1,0:T(8,128)(2,1)} %param.7), kind=kOutput, calls=%fused_computation.2 | convolution fusion | flops 4834981888 | bytes 14168064 | tf_op jit(solution)/shard_map/dot_general | solution.py:53
  128.1 9.1 %psum.28 = f32[2,1024]{1,0:T(2,128)S(1)} all-reduce(f32[2,1024]{1,0:T(2,128)S(1)} %pad_maximum_fusion), channel_id=1, replica_groups=mesh['tok_0'=4,'tok_1'=2,'voc_0'=8,'voc_1'=8] {'tok_0'}, use_global_device_ids=true, to_apply=%region_3.4 | all-reduce | flops 2048 | bytes 16384 | tf_op jit(solution)/shard_map/psum | solution.py:37
  137.2 2.5 %psum.29 = f32[2,1024]{1,0:T(2,128)S(1)} all-reduce(f32[2,1024]{1,0:T(2,128)S(1)} %psum.28), channel_id=1, replica_groups=mesh['tok_0'=4,'tok_1'=2,'voc_0'=8,'voc_1'=8] {'tok_1'}, use_global_device_ids=true, to_apply=%region_4.5 | all-reduce | flops 2048 | bytes 16384 | tf_op jit(solution)/shard_map/psum | solution.py:37
  139.7 18.3 %psum.30 = f32[2,1024]{1,0:T(2,128)S(1)} all-reduce(f32[2,1024]{1,0:T(2,128)S(1)} %psum.29), channel_id=1, replica_groups=mesh['tok_0'=4,'tok_1'=2,'voc_0'=8,'voc_1'=8] {'voc_0'}, use_global_device_ids=true, to_apply=%region_5.6 | all-reduce | flops 2048 | bytes 16384 | tf_op jit(solution)/shard_map/psum | solution.py:37
  158.1 17.2 %psum.31 = f32[2,1024]{1,0:T(2,128)S(1)} all-reduce(f32[2,1024]{1,0:T(2,128)S(1)} %psum.30), channel_id=1, replica_groups=mesh['tok_0'=4,'tok_1'=2,'voc_0'=8,'voc_1'=8] {'voc_1'}, use_global_device_ids=true, to_apply=%region_6.7 | all-reduce | flops 2048 | bytes 16384 | tf_op jit(solution)/shard_map/psum | solution.py:37
  175.3 0.6 select_reduce_fusion.1
  175.9 0.6 dynamic_slice.3
  (4 shorter events, 0.0 us)
Async XLA Ops:
  7.2 111.5 %all-gather.2.cloned.1.call-start = ((), (), s32[]{:S(2)}) async-start(), calls=%async_computation.2 | async-start | bytes 10616832 | tf_op jit(solution)/shard_map/all_gather | solution.py:54
  66.6 1.3 copy-start.1
  66.6 2.3 %copy-start = (s32[1024]{0:T(1024)S(1)}, s32[1024]{0:T(1024)}, u32[]{:S(2)}) copy-start(s32[1024]{0:T(1024)} %param.8) | copy-start | bytes 12292
Sparse Core Ops, SparseCore 0:
  68.1 50.4 all-gather.1
